TPU v7x, 128 devices: a whole 4x4x4 slice. The times are simulated.
128 devices in a mesh: rep: 1, tp: 2 (over core), dp: 64 (over z, y, x).
Axes of the slice: x: 4, y: 4, z: 4, core: 2. Of those that a mesh axis runs over, the one named last changes fastest.
Arguments:
- x: bfloat16 [128, 2560], P(('rep', 'dp'))
- lengths: int32 [128], P(('rep', 'dp'))
- cache0: bfloat16 [128, 4096, 288], P(('rep', 'dp'))
- cache1: bfloat16 [128, 4096, 288], P(('rep', 'dp'))
- attn_gain: float32 [2, 2560], replicated
- kv_gain: float32 [2, 256], replicated
- q_gain: float32 [2, 768], replicated
- ffn_gain: float32 [2, 2560], replicated
- w_dkv: bfloat16 [2, 2560, 288], replicated
- w_qa: bfloat16 [2, 2560, 768], replicated
- w_qb: bfloat16 [2, 768, 3840], P(None, None, 'tp')
- w_uk: bfloat16 [2, 40, 64, 256], P(None, 'tp')
- w_uv: bfloat16 [2, 40, 256, 64], P(None, 'tp')
- w_o: bfloat16 [2, 2560, 2560], P(None, 'tp')
- w_gate: bfloat16 [2, 2560, 6400], replicated
- w_up: bfloat16 [2, 2560, 6400], replicated
- w_down: bfloat16 [2, 6400, 2560], replicated
Outputs:
- output 1: bfloat16 [128, 2560], P(('rep', 'dp'))
- output 2: bfloat16 [128, 4096, 288], P(('rep', 'dp'))
- output 3: bfloat16 [128, 4096, 288], P(('rep', 'dp'))
All inputs are finite; a program needn't handle non-finite values.
Results may differ from a plain program's by a relative error of at most 0.0143243.
Values are sent between devices in bfloat16 or wider.
A program may use at most 1 GiB of HBM per device.

v0:
```python
import jax
import jax.numpy as jnp
from jax import lax
from jax.sharding import PartitionSpec as P

NORM_EPS = 1e-6
ROPE_BASE = 10000.0


def rms_norm(values, gain_vec):
    wide_vals = values.astype(jnp.float32)
    inv_rms = lax.rsqrt(jnp.mean(wide_vals * wide_vals, axis=-1, keepdims=True) + NORM_EPS)
    return (wide_vals * inv_rms * gain_vec).astype(jnp.bfloat16)


def rope_tables(lengths, rope_dim):
    half_dim = rope_dim // 2
    inv_freq = ROPE_BASE ** (-2.0 * jnp.arange(half_dim).astype(jnp.float32) / rope_dim)
    angles = lengths.astype(jnp.float32)[:, None] * inv_freq[None, :]
    return jnp.cos(angles), jnp.sin(angles)


def rotate(values, cos_tab, sin_tab):
    half_dim = values.shape[-1] // 2
    first_half = values[..., :half_dim]
    second_half = values[..., half_dim:]
    return jnp.concatenate([first_half * cos_tab - second_half * sin_tab, second_half * cos_tab + first_half * sin_tab], axis=-1)


def attention_local(x_rows, lengths, cache, cos_tab, sin_tab, attn_g, kv_g, q_g, w_dkv, w_qa, w_qb, w_uk, w_uv, w_o):
    row_count = x_rows.shape[0]
    head_count, nope_dim, value_a7 = w_uk.shape
    qk_width = w_qb.shape[1] // head_count
    slot_ids = jnp.arange(cache.shape[1])
    normed = rms_norm(x_rows, attn_g)
    kv_lat = jnp.dot(normed, w_dkv, preferred_element_type=jnp.float32)
    new_entry = jnp.concatenate([rms_norm(kv_lat[:, :value_a7], kv_g), rotate(kv_lat[:, value_a7:], cos_tab, sin_tab).astype(jnp.bfloat16)], axis=-1)
    is_slot = (slot_ids[None, :] == lengths[:, None])[:, :, None]
    new_cache = jnp.where(is_slot, new_entry[:, None, :], cache)
    q_low = rms_norm(jnp.dot(normed, w_qa, preferred_element_type=jnp.float32), q_g)
    q_full = jnp.dot(q_low, w_qb, preferred_element_type=jnp.float32).reshape(row_count, head_count, qk_width)
    q_nope = q_full[:, :, :nope_dim].astype(jnp.bfloat16)
    q_rot = rotate(q_full[:, :, nope_dim:], cos_tab[:, None, :], sin_tab[:, None, :]).astype(jnp.bfloat16)
    q_lat = jnp.einsum('bhn,hnk->bhk', q_nope, w_uk, preferred_element_type=jnp.float32).astype(jnp.bfloat16)
    query_vec = jnp.concatenate([q_lat, q_rot], axis=-1)
    scores = jnp.einsum('bhk,btk->bht', query_vec, new_cache, preferred_element_type=jnp.float32) * qk_width ** -0.5
    valid_mask = (slot_ids[None, :] <= lengths[:, None])[:, None, :]
    att_probs = jax.nn.softmax(jnp.where(valid_mask, scores, -1e30), axis=-1).astype(jnp.bfloat16)
    lat_out = jnp.einsum('bht,btk->bhk', att_probs, new_cache, preferred_element_type=jnp.float32)[:, :, :value_a7].astype(jnp.bfloat16)
    head_out = jnp.einsum('cil,ilw->ciw', lat_out, w_uv, preferred_element_type=jnp.float32).astype(jnp.bfloat16)
    attn_part = jnp.dot(head_out.reshape(row_count, head_count * w_uv.shape[2]), w_o, preferred_element_type=jnp.float32)
    return attn_part, new_cache


def solution(mesh):
    tp_size = mesh.shape['tp']
    dp_size = mesh.shape['dp']
    row_spec = P(('rep', 'dp'), None)
    cache_spec = P(('rep', 'dp'), None, None)
    in_specs = (row_spec, P(('rep', 'dp')), cache_spec, cache_spec, P(), P(), P(), P(), P(), P(), P(None, None, 'tp'), P(None, 'tp', None, None), P(None, 'tp', None, None), P(None, 'tp', None), P(), P(), P())
    out_specs = (row_spec, cache_spec, cache_spec)

    def local_step(x, lengths, cache0, cache1, attn_gain, kv_gain, q_gain, ffn_gain, w_dkv, w_qa, w_qb, w_uk, w_uv, w_o, w_gate, w_up, w_down):
        row_count, model_dim = x.shape
        ffn_width = w_gate.shape[2] // (tp_size * dp_size)
        ffn_start = (lax.axis_index('tp') * dp_size + lax.axis_index('dp')) * ffn_width
        rope_dim = cache0.shape[2] - w_uk.shape[3]
        cos_tab, sin_tab = rope_tables(lengths, rope_dim)
        caches = [cache0, cache1]
        new_caches = []
        x_rows = x
        for layer_idx in range(len(caches)):
            attn_part, new_cache = attention_local(x_rows, lengths, caches[layer_idx], cos_tab, sin_tab, attn_gain[layer_idx], kv_gain[layer_idx], q_gain[layer_idx], w_dkv[layer_idx], w_qa[layer_idx], w_qb[layer_idx], w_uk[layer_idx], w_uv[layer_idx], w_o[layer_idx])
            attn_out = lax.psum(attn_part, 'tp')
            x_mid = (x_rows.astype(jnp.float32) + attn_out).astype(jnp.bfloat16)
            ffn_in = rms_norm(x_mid, ffn_gain[layer_idx])
            all_in = lax.all_gather(ffn_in, 'dp', axis=0, tiled=True)
            gate_cols = lax.dynamic_slice(w_gate, (layer_idx, 0, ffn_start), (1, model_dim, ffn_width))[0]
            up_cols = lax.dynamic_slice(w_up, (layer_idx, 0, ffn_start), (1, model_dim, ffn_width))[0]
            down_rows = lax.dynamic_slice(w_down, (layer_idx, ffn_start, 0), (1, ffn_width, model_dim))[0]
            hidden = (jax.nn.silu(jnp.dot(all_in, gate_cols, preferred_element_type=jnp.float32)) * jnp.dot(all_in, up_cols, preferred_element_type=jnp.float32)).astype(jnp.bfloat16)
            ffn_partial = jnp.dot(hidden, down_rows, preferred_element_type=jnp.float32).astype(jnp.bfloat16)
            received = lax.all_to_all(ffn_partial, 'dp', 0, 0, tiled=True)
            rank_sum = jnp.sum(received.reshape(dp_size, row_count, model_dim).astype(jnp.float32), axis=0)
            ffn_out = lax.psum(rank_sum, 'tp')
            x_rows = (x_mid.astype(jnp.float32) + ffn_out).astype(jnp.bfloat16)
            new_caches.append(new_cache)
        return x_rows, new_caches[0], new_caches[1]

    return jax.shard_map(local_step, mesh=mesh, in_specs=in_specs, out_specs=out_specs, check_vma=False)
```

profile of v0, /device:TPU:1, one launch (start us, length us, event | category | flops | bytes accessed | tf_op | source)
XLA Modules:
  0.0 482.7 jit_solution(5874519661382676086)
XLA Ops:
  0.6 0.7 convert_element_type.123
  1.3 0.8 iota_compare_fusion.1
  2.1 0.9 slice_reduce_fusion.1
  2.9 0.8 fusion.74
  3.8 2.9 multiply_reduce_fusion.1
  6.7 4.8 slice_bitcast_fusion
  11.5 4.5 copy.34
  16.0 1.9 fusion.22
  17.9 0.1 multiply_reduce_fusion.3
  18.1 0.1 subtract_convert_fusion.3
  18.2 2.8 fusion.98
  21.0 1.3 fusion.28
  22.3 0.1 subtract_convert_fusion.1
  22.5 0.1 pad_maximum_fusion
  22.7 2.7 broadcast_select_fusion.1
  25.5 0.9 fusion.13
  26.4 1.3 copy-done
  27.6 0.9 copy-done.3
  28.5 0.3 fusion.121
  28.8 4.3 fusion.54
  33.1 1.4 fusion.30
  34.5 0.1 reshape.181
  34.6 3.8 fusion.4
  38.4 4.6 psum.28
  43.0 0.1 fusion.78
  43.3 153.8 %all-gather = bf16[64,2,2560]{2,1,0:T(2,128)(2,1)} all-gather(bf16[1,2,2560]{2,1,0:T(2,128)(2,1)S(1)} %fusion.95), channel_id=1, replica_groups=mesh['rep'=1,'tp'=2,'dp'=64] {'dp'}, dimensions={0}, use_global_device_ids=true | all-gather | bytes 665600 | tf_op jit(solution)/shard_map/all_gather | solution.py:77
  197.1 2.7 reshape.184
  199.8 2.2 fusion.40
  202.0 3.7 convolution_convert_fusion.1
  205.8 2.6 all_to_all.12
  208.4 5.5 %all-to-all-start = ((bf16[64,2,2560]{2,1,0:T(2,128)(2,1)}), bf16[64,2,2560]{2,1,0:T(2,128)(2,1)}, u32[]{:S(2)}, u32[]{:S(2)}) async-start(bf16[64,2,2560]{2,1,0:T(2,128)(2,1)} %all_to_all.12), calls=%async_computation | async-start | bytes 1310720 | tf_op jit(solution)/shard_map/all_to_all | solution.py:83
  213.8 2.8 copy.38
  216.6 8.3 %all-to-all-done = bf16[64,2,2560]{2,1,0:T(2,128)(2,1)} async-done(((bf16[64,2,2560]{2,1,0:T(2,128)(2,1)}), bf16[64,2,2560]{2,1,0:T(2,128)(2,1)}, u32[]{:S(2)}, u32[]{:S(2)}) %all-to-all-start) | async-done | bytes 655392 | tf_op jit(solution)/shard_map/all_to_all | solution.py:83
  224.9 1.6 convert_reduce_fusion.1
  226.5 32.8 %psum.29 = f32[2,2560]{1,0:T(2,128)S(1)} all-reduce(f32[2,2560]{1,0:T(2,128)S(1)} %convert_reduce_fusion.1), channel_id=1, replica_groups=mesh['rep'=1,'tp'=2,'dp'=64] {'tp'}, use_global_device_ids=true, to_apply=%region_8.9 | all-reduce | flops 5120 | bytes 40960 | tf_op jit(solution)/shard_map/psum | solution.py:85
  259.3 0.1 fusion.82
  259.5 3.0 multiply_reduce_fusion
  262.6 1.0 fusion.96
  263.5 0.1 subtract_convert_fusion
  263.7 0.2 fusion.29
  263.9 0.5 fusion.20
  264.4 0.1 multiply_reduce_fusion.2
  264.5 0.1 subtract_convert_fusion.2
  264.8 2.7 broadcast_select_fusion
  267.6 0.1 pad_maximum_fusion.1
  267.7 0.9 fusion.12
  268.6 1.2 copy-done.1
  269.8 0.3 fusion.122
  270.1 3.8 fusion.55
  274.0 0.3 fusion.31
  274.2 0.1 reshape.182
  274.3 3.8 fusion.2
  278.2 3.5 psum.30
  281.7 0.1 fusion.86
  281.8 0.1 fusion.94
  281.9 146.8 %all-gather.1 = bf16[64,2,2560]{2,1,0:T(2,128)(2,1)S(1)} all-gather(bf16[1,2,2560]{2,1,0:T(2,128)(2,1)S(1)} %fusion.94), channel_id=1, replica_groups=mesh['rep'=1,'tp'=2,'dp'=64] {'dp'}, dimensions={0}, use_global_device_ids=true | all-gather | bytes 665600 | tf_op jit(solution)/shard_map/all_gather | solution.py:77
  428.7 0.2 reshape.186
  428.9 2.0 fusion.34
  431.0 2.7 convolution_convert_fusion
  433.6 0.2 all_to_all.14
  433.9 15.4 %all_to_all.18 = bf16[64,2,2560]{2,1,0:T(2,128)(2,1)S(1)} all-to-all(bf16[64,2,2560]{2,1,0:T(2,128)(2,1)S(1)} %all_to_all.14), channel_id=1, replica_groups=mesh['rep'=1,'tp'=2,'dp'=64] {'dp'}, dimensions={0} | all-to-all | bytes 1310720 | tf_op jit(solution)/shard_map/all_to_all | solution.py:83
  449.3 0.5 convert_reduce_fusion
  449.9 32.3 %psum.31 = f32[2,2560]{1,0:T(2,128)S(1)} all-reduce(f32[2,2560]{1,0:T(2,128)S(1)} %convert_reduce_fusion), channel_id=1, replica_groups=mesh['rep'=1,'tp'=2,'dp'=64] {'tp'}, use_global_device_ids=true, to_apply=%region_17.18 | all-reduce | flops 5120 | bytes 40960 | tf_op jit(solution)/shard_map/psum | solution.py:85
  482.1 0.6 fusion.89
  (40 shorter events, 0.7 us)
Async XLA Ops:
  11.5 4.5 copy-start.7
  11.5 4.6 copy-start.5
  11.5 6.6 %copy-start.8 = (f32[2,256]{1,0:T(2,128)S(1)}, f32[2,256]{1,0:T(2,128)}, u32[]{:S(2)}) copy-start(f32[2,256]{1,0:T(2,128)} %param.22) | copy-start | bytes 6148
  25.4 2.2 copy-start
  27.6 0.9 copy-start.3
  33.1 10.1 %copy-start.6 = (f32[2,2560]{1,0:T(2,128)S(1)}, f32[2,2560]{1,0:T(2,128)}, u32[]{:S(2)}) copy-start(f32[2,2560]{1,0:T(2,128)} %param.24) | copy-start | bytes 61444
  208.4 16.5 %all-to-all-start = ((bf16[64,2,2560]{2,1,0:T(2,128)(2,1)}), bf16[64,2,2560]{2,1,0:T(2,128)(2,1)}, u32[]{:S(2)}, u32[]{:S(2)}) async-start(bf16[64,2,2560]{2,1,0:T(2,128)(2,1)} %all_to_all.12), calls=%async_computation | async-start | bytes 1310720 | tf_op jit(solution)/shard_map/all_to_all | solution.py:83
  216.6 45.9 %copy-start.2 = (bf16[1920,768]{1,0:T(8,128)(2,1)S(1)}, bf16[1920,768]{1,0:T(8,128)(2,1)}, u32[]{:S(2)}) copy-start(bf16[1920,768]{1,0:T(8,128)(2,1)} %copy.38) | copy-start | bytes 8847364
  259.3 4.4 copy-start.4
  259.3 4.6 copy-start.9
  267.6 2.2 copy-start.1
  269.8 4.2 copy-start.10
where the time goes:
time: 484 us; the launch traced here: 483 us
  blocking collectives  389 us (80%)
  matrix products  43.4 us (9%)
  local copies, waits for them, and re-layouts  22.5 us (5%)
  other arithmetic  13 us (3%)
  waiting for transfers between devices  8.27 us (2%)
  starting transfers between devices  5.46 us (1%)
    all_gather x2, blocking collectives, local_step(): all_in = lax.all_gather(ffn_in, 'dp', axis=0, tiled=True)  301 us
    psum x2, blocking collectives, local_step(): ffn_out = lax.psum(rank_sum, 'tp')  65 us
    all_to_all x1, blocking collectives, local_step(): received = lax.all_to_all(ffn_partial, 'dp', 0, 0, tiled=True)  15.4 us
    dot_general x3, local copies, waits for them, and re-layouts, attention_local(): jnp.dot(q_low, w_qb, preferred_element_type=jnp.float32)  12.1 us
  transfers between devices with their start and end apart: 1, of which 1 were waited for; matrix products, arithmetic and copies ran while one was open for 1% of the time, Pallas kernels for 0%

commit v1 on v0

v1 whole, which is shorter than its diff:
```python
import functools

import jax
import jax.numpy as jnp
import numpy as np
from jax import lax
from jax.experimental import pallas as pl
from jax.experimental.pallas import tpu as pltpu
from jax.sharding import PartitionSpec as P

MESH = pl.DeviceIdType.MESH
NORM_EPS = 1e-6
ROPE_BASE = 10000.0
HEAD_PAD = 24
LANES = 128
VMEM_SPEC = pl.BlockSpec(memory_space=pltpu.VMEM)
SMEM_SPEC = pl.BlockSpec(memory_space=pltpu.SMEM)
ANY_SPEC = pl.BlockSpec(memory_space=pltpu.HBM)
NT = (((1,), (1,)), ((), ()))


def dot(a, b):
    return jnp.dot(a, b, preferred_element_type=jnp.float32)


def dot_nt(a, b):
    return lax.dot_general(a, b, NT, preferred_element_type=jnp.float32)


def rms(values, gain):
    inv = lax.rsqrt(jnp.mean(values * values, axis=-1, keepdims=True) + NORM_EPS)
    return (values * inv * gain).astype(jnp.bfloat16)


def rope_freq(head_width, nope, rope, width):
    half = rope // 2
    inv = ROPE_BASE ** (-2.0 * np.arange(half) / rope)
    freq = np.zeros(width + LANES)
    sign = np.zeros(width + LANES)
    starts = [h * head_width + nope for h in range(width // head_width)] + [width]
    for s in starts:
        freq[s:s + half] = inv
        freq[s + half:s + rope] = inv
        sign[s:s + half] = -1.0
        sign[s + half:s + rope] = 1.0
    return freq.astype(np.float32), sign.astype(np.float32)


def rotate_lanes(values, cos, sin, half):
    width = values.shape[-1]
    up = pltpu.roll(values, width - half, 1)
    down = pltpu.roll(values, half, 1)
    lane = lax.broadcasted_iota(jnp.int32, values.shape, 1)
    return values, up, down, lane


def attn_kernel(layer, dims, len_ref, x_ref, tab_ref, attn_g, kv_g, q_g, cache, w_dkv, w_qa, w_qb, w_uk, w_uv, w_o, part_ref, cache_out,
                dkv_b, qa_b, qb_b, uk_b, uv_b, o_b, c_b, s_b, p_b, sems, out_sems):
    rows, heads, nope, rope, lat, slots = dims
    half = rope // 2
    width = heads * (nope + rope)
    hw = nope + rope
    entry_w = lat + rope

    copies = {}

    def begin(name, src, dst, i):
        copies[name] = pltpu.make_async_copy(src, dst, sems.at[i])
        copies[name].start()

    qa_rows = w_qa.shape[1] // 2
    qb_rows = w_qb.shape[1] // 2
    o_rows = w_o.shape[1] // 4
    begin("dkv", w_dkv.at[layer], dkv_b, 0)
    for i in range(2):
        begin(f"qa{i}", w_qa.at[layer, pl.ds(i * qa_rows, qa_rows)], qa_b.at[pl.ds(i * qa_rows, qa_rows)], 1 + i)
    for i in range(2):
        begin(f"qb{i}", w_qb.at[layer, pl.ds(i * qb_rows, qb_rows)], qb_b.at[pl.ds(i * qb_rows, qb_rows)], 3 + i)
    begin("uk", w_uk.at[layer], uk_b.at[:, pl.ds(0, nope), pl.ds(0, lat)], 5)
    for r in range(rows):
        begin(f"c{r}", cache.at[r], c_b.at[r], 6 + r)
    begin("uv", w_uv.at[layer], uv_b, 8)
    for i in range(4):
        begin(f"o{i}", w_o.at[layer, pl.ds(i * o_rows, o_rows)], o_b.at[pl.ds(i * o_rows, o_rows)], 9 + i)

    uk_b[:, nope:, :lat] = jnp.zeros((heads, rope, lat), jnp.bfloat16)
    sub = lax.broadcasted_iota(jnp.int32, (heads, hw, LANES), 1)
    lan = lax.broadcasted_iota(jnp.int32, (heads, hw, LANES), 2)
    uk_b[:, :, lat:] = jnp.where(sub == lan + nope, 1.0, 0.0).astype(jnp.bfloat16)

    h = rms(x_ref[...].astype(jnp.float32), attn_g[layer:layer + 1, :])
    cos, sin = tab_ref[0], tab_ref[1]

    copies["dkv"].wait()
    kv = dot_nt(h, dkv_b[...])
    k_lat = rms(kv[:, :lat], kv_g[layer:layer + 1, :])
    k_raw = jnp.concatenate([kv[:, lat:], jnp.zeros((rows, LANES - rope), jnp.float32)], axis=1)
    lane = lax.broadcasted_iota(jnp.int32, k_raw.shape, 1)
    k_other = jnp.where(lane < half, pltpu.roll(k_raw, LANES - half, 1), pltpu.roll(k_raw, half, 1))
    k_rot = (k_raw * cos[:, width:] + k_other * sin[:, width:]).astype(jnp.bfloat16)
    entry = jnp.concatenate([k_lat.astype(jnp.float32), k_rot.astype(jnp.float32)], axis=1)
    entry = jnp.concatenate([entry, jnp.zeros((8 - rows, lat + LANES), jnp.float32)], axis=0)
    entry_t = entry.T[:entry_w]

    qa = jnp.zeros((rows, w_qa.shape[2]), jnp.float32)
    for i in range(2):
        copies[f"qa{i}"].wait()
        qa += dot(h[:, i * qa_rows:(i + 1) * qa_rows], qa_b[pl.ds(i * qa_rows, qa_rows)])
    q_low = rms(qa, q_g[layer:layer + 1, :])
    q = jnp.zeros((rows, width), jnp.float32)
    for i in range(2):
        copies[f"qb{i}"].wait()
        q += dot(q_low[:, i * qb_rows:(i + 1) * qb_rows], qb_b[pl.ds(i * qb_rows, qb_rows)])
    sin_q = sin[:, :width]
    q_other = jnp.where(sin_q < 0, 1.0, 0.0)
    lane = lax.broadcasted_iota(jnp.int32, q.shape, 1) % hw
    q_other = jnp.where(lane < nope + half, pltpu.roll(q, width - half, 1), pltpu.roll(q, half, 1))
    q = jnp.where(lane < nope, q, q * cos[:, :width] + q_other * sin_q)

    spread_shape = (HEAD_PAD, width)
    own = lax.broadcasted_iota(jnp.int32, spread_shape, 0) == lax.broadcasted_iota(jnp.int32, spread_shape, 1) // hw
    spread = jnp.concatenate([jnp.where(own, jnp.broadcast_to(q[r:r + 1], spread_shape), 0.0) for r in range(rows)], axis=0).astype(jnp.bfloat16)
    copies["uk"].wait()
    query = dot(spread, uk_b[...].reshape(width, lat + LANES))

    chunk = 1024
    pieces = slots // chunk
    scale = hw ** -0.5
    o_lat = []
    for r in range(rows):
        copies[f"c{r}"].wait()
        length = len_ref[r]
        base = pl.multiple_of(length // LANES * LANES, LANES)
        tile = c_b[r, :, pl.ds(base, LANES)].astype(jnp.float32)
        lane = lax.broadcasted_iota(jnp.int32, tile.shape, 1)
        tile = jnp.where(lane == length - base, jnp.broadcast_to(entry_t[:, r:r + 1], tile.shape), tile)
        c_b[r, :, pl.ds(base, LANES)] = tile.astype(jnp.bfloat16)

        q_r = query[r * HEAD_PAD:(r + 1) * HEAD_PAD].astype(jnp.bfloat16)
        top = jnp.full((HEAD_PAD, 1), -1e30, jnp.float32)
        for c in range(pieces):
            cols = pl.ds(c * chunk, chunk)
            s = dot(q_r[:, :lat], c_b[r, pl.ds(0, lat), cols]) + dot(q_r[:, lat:entry_w], c_b[r, pl.ds(lat, rope), cols])
            slot = lax.broadcasted_iota(jnp.int32, s.shape, 1) + c * chunk
            s = jnp.where(slot <= length, s * scale, -1e30)
            s_b[r, :, cols] = s
            top = jnp.maximum(top, jnp.max(s, axis=1, keepdims=True))
        copies[f"out{r}"] = pltpu.make_async_copy(c_b.at[r], cache_out.at[r], out_sems.at[r])
        copies[f"out{r}"].start()
        total = jnp.zeros((HEAD_PAD, 1), jnp.float32)
        for c in range(pieces):
            cols = pl.ds(c * chunk, chunk)
            e = jnp.exp(s_b[r, :, cols] - top)
            s_b[r, :, cols] = e
            total += jnp.sum(e, axis=1, keepdims=True)
        inv = 1.0 / total
        acc = jnp.zeros((HEAD_PAD, lat), jnp.float32)
        for c in range(pieces):
            cols = pl.ds(c * chunk, chunk)
            p = (s_b[r, :, cols] * inv).astype(jnp.bfloat16)
            acc += dot_nt(p, c_b[r, pl.ds(0, lat), cols])
        o_lat.append(acc)

    o_lat = jnp.concatenate(o_lat, axis=0).astype(jnp.bfloat16)
    copies["uv"].wait()
    v_dim = w_uv.shape[2]
    wide = dot_nt(o_lat, uv_b[...].reshape(heads * v_dim, lat))
    pick_shape = (HEAD_PAD, heads * v_dim)
    own = lax.broadcasted_iota(jnp.int32, pick_shape, 0) == lax.broadcasted_iota(jnp.int32, pick_shape, 1) // v_dim
    o = [jnp.sum(jnp.where(own, wide[r * HEAD_PAD:(r + 1) * HEAD_PAD], 0.0), axis=0, keepdims=True) for r in range(rows)]
    o = jnp.concatenate(o, axis=0).astype(jnp.bfloat16)
    part = jnp.zeros(part_ref.shape, jnp.float32)
    for i in range(4):
        copies[f"o{i}"].wait()
        part += dot(o[:, i * o_rows:(i + 1) * o_rows], o_b[pl.ds(i * o_rows, o_rows)])
    part_ref[...] = part
    for r in range(rows):
        copies[f"out{r}"].wait()


def attention(layer, lengths, x, tables, attn_gain, kv_gain, q_gain, cache_t, w_dkv_t, w_qa, w_qb, w_uk, w_uv_t, w_o):
    rows, model = x.shape
    heads, nope, lat = w_uk.shape[1:]
    slots = cache_t.shape[2]
    rope = cache_t.shape[1] - lat
    bf = jnp.bfloat16
    width = w_qb.shape[2]
    dims = (rows, heads, nope, rope, lat, slots)
    return pl.pallas_call(
        functools.partial(attn_kernel, layer, dims),
        name=f"attn{layer}",
        out_shape=(jax.ShapeDtypeStruct((rows, model), jnp.float32), jax.ShapeDtypeStruct(cache_t.shape, bf)),
        in_specs=[SMEM_SPEC] + [VMEM_SPEC] * 5 + [ANY_SPEC] * 7,
        out_specs=(VMEM_SPEC, ANY_SPEC),
        scratch_shapes=[
            pltpu.VMEM(w_dkv_t.shape[1:], bf),
            pltpu.VMEM(w_qa.shape[1:], bf),
            pltpu.VMEM(w_qb.shape[1:], bf),
            pltpu.VMEM((heads, nope + rope, lat + LANES), bf),
            pltpu.VMEM(w_uv_t.shape[1:], bf),
            pltpu.VMEM(w_o.shape[1:], bf),
            pltpu.VMEM(cache_t.shape, bf),
            pltpu.VMEM((rows, HEAD_PAD, slots), jnp.float32),
            pltpu.VMEM((8, LANES), bf),
            pltpu.SemaphoreType.DMA((13,)),
            pltpu.SemaphoreType.DMA((2,)),
        ],
        compiler_params=pltpu.CompilerParams(vmem_limit_bytes=62 * 2 ** 20),
        cost_estimate=pl.CostEstimate(flops=2 * 10 ** 8, bytes_accessed=26 * 10 ** 6, transcendentals=2 * 10 ** 5),
    )(lengths, x, tables, attn_gain, kv_gain, q_gain, cache_t, w_dkv_t, w_qa, w_qb, w_uk, w_uv_t, w_o)


def ffn_kernel(layer, dims, part_ref, x_ref, ffn_g, w_gate, w_up, w_down, out_ref,
               gate_b, up_b, down_b, mine_b, part_b, mid_b, send_b, sum_b, w_sems, s1, r1, s2, r2):
    ranks, tp, rows, tiles_all, tiles = dims
    members = ranks * tp
    c = lax.axis_index("tp")
    d = lax.axis_index("dp")
    pos = lax.rem(d, ranks)
    base = d - pos
    me = pos * tp + c
    start = tiles_all * me // members
    count = tiles_all * (me + 1) // members - start
    first = pl.multiple_of(jnp.minimum(start, tiles_all - tiles) * LANES, LANES)
    skip = start - jnp.minimum(start, tiles_all - tiles)

    loads = [
        pltpu.make_async_copy(w_gate.at[layer, :, pl.ds(first, tiles * LANES)], gate_b, w_sems.at[0]),
        pltpu.make_async_copy(w_up.at[layer, :, pl.ds(first, tiles * LANES)], up_b, w_sems.at[1]),
        pltpu.make_async_copy(w_down.at[layer, pl.ds(first, tiles * LANES)], down_b, w_sems.at[2]),
    ]
    for load in loads:
        load.start()

    def peer(k):
        other = lax.rem(me + k, members)
        return other // tp, lax.rem(other, tp)

    barrier = pltpu.get_barrier_semaphore()
    for k in range(1, members):
        q, t = peer(k)
        pl.semaphore_signal(barrier, inc=1, device_id={"tp": t, "dp": base + q}, device_id_type=MESH)

    keep = jnp.where(c == 0, 1.0, 0.0)
    mine = part_ref[...] + x_ref[...].astype(jnp.float32) * keep
    mine_b[...] = mine
    part_b[me] = mine
    pl.semaphore_wait(barrier, members - 1)

    sends = []
    for k in range(1, members):
        q, t = peer(k)
        sends.append(pltpu.make_async_remote_copy(
            src_ref=mine_b, dst_ref=part_b.at[me], send_sem=s1.at[k - 1], recv_sem=r1.at[k - 1],
            device_id={"tp": t, "dp": base + q}, device_id_type=MESH))
    for copy in sends:
        copy.start()
    for copy in sends:
        copy.wait_recv()

    for q in range(ranks):
        total = part_b[q * tp]
        for t in range(1, tp):
            total = total + part_b[q * tp + t]
        mid_b[q * rows:(q + 1) * rows, :] = total.astype(jnp.bfloat16).astype(jnp.float32)
    g = rms(mid_b[...], ffn_g[layer:layer + 1, :])
    loads[0].wait()
    a = dot(g, gate_b[...])
    loads[1].wait()
    b = dot(g, up_b[...])
    lane = lax.broadcasted_iota(jnp.int32, a.shape, 1)
    kept = (lane >= skip * LANES) & (lane < (skip + count) * LANES)
    u = jnp.where(kept, a * jax.nn.sigmoid(a) * b, 0.0).astype(jnp.bfloat16)
    loads[2].wait()
    partial = dot(u, down_b[...])
    for q in range(ranks):
        send_b[q] = partial[q * rows:(q + 1) * rows].astype(jnp.bfloat16)
    sum_b[me] = send_b[pos]

    returns = []
    for k in range(1, members):
        q, t = peer(k)
        returns.append(pltpu.make_async_remote_copy(
            src_ref=send_b.at[q], dst_ref=sum_b.at[me], send_sem=s2.at[k - 1], recv_sem=r2.at[k - 1],
            device_id={"tp": t, "dp": base + q}, device_id_type=MESH))
    for copy in returns:
        copy.start()
    own = part_b[pos * tp]
    for t in range(1, tp):
        own = own + part_b[pos * tp + t]
    own = own.astype(jnp.bfloat16).astype(jnp.float32)
    for copy in returns:
        copy.wait_recv()
    total = sum_b[0].astype(jnp.float32)
    for j in range(1, members):
        total = total + sum_b[j].astype(jnp.float32)
    out_ref[...] = (own + total).astype(jnp.bfloat16)
    for copy in sends + returns:
        copy.wait_send()


def ffn(layer, ranks, tp, part, x, ffn_gain, w_gate, w_up, w_down):
    rows, model = x.shape
    tiles_all = w_gate.shape[2] // LANES
    members = ranks * tp
    tiles = -(-tiles_all // members)
    width = tiles * LANES
    bf = jnp.bfloat16
    return pl.pallas_call(
        functools.partial(ffn_kernel, layer, (ranks, tp, rows, tiles_all, tiles)),
        name=f"ffn{layer}",
        out_shape=jax.ShapeDtypeStruct((rows, model), bf),
        in_specs=[VMEM_SPEC] * 3 + [ANY_SPEC] * 3,
        out_specs=VMEM_SPEC,
        scratch_shapes=[
            pltpu.VMEM((model, width), bf),
            pltpu.VMEM((model, width), bf),
            pltpu.VMEM((width, model), bf),
            pltpu.VMEM((rows, model), jnp.float32),
            pltpu.VMEM((members, rows, model), jnp.float32),
            pltpu.VMEM((ranks * rows, model), jnp.float32),
            pltpu.VMEM((ranks, rows, model), bf),
            pltpu.VMEM((members, rows, model), bf),
            pltpu.SemaphoreType.DMA((3,)),
            pltpu.SemaphoreType.DMA((members - 1,)),
            pltpu.SemaphoreType.DMA((members - 1,)),
            pltpu.SemaphoreType.DMA((members - 1,)),
            pltpu.SemaphoreType.DMA((members - 1,)),
        ],
        compiler_params=pltpu.CompilerParams(collective_id=layer, has_side_effects=True, vmem_limit_bytes=32 * 2 ** 20),
        cost_estimate=pl.CostEstimate(flops=2 * 10 ** 8, bytes_accessed=14 * 10 ** 6, transcendentals=10 ** 4),
    )(part, x, ffn_gain, w_gate, w_up, w_down)


def solution(mesh):
    tp_size = mesh.shape['tp']
    ranks = 4
    row_spec = P(('rep', 'dp'), None)
    cache_spec = P(('rep', 'dp'), None, None)
    in_specs = (row_spec, P(('rep', 'dp')), cache_spec, cache_spec, P(), P(), P(), P(), P(), P(), P(None, None, 'tp'), P(None, 'tp', None, None), P(None, 'tp', None, None), P(None, 'tp', None), P(), P(), P())
    out_specs = (row_spec, cache_spec, cache_spec)

    def local_step(x, lengths, cache0, cache1, attn_gain, kv_gain, q_gain, ffn_gain, w_dkv, w_qa, w_qb, w_uk, w_uv, w_o, w_gate, w_up, w_down):
        nope, lat = w_uk.shape[2:]
        rope = cache0.shape[2] - lat
        freq, sign = rope_freq(nope + rope, nope, rope, w_qb.shape[2])
        angles = lengths.astype(jnp.float32)[:, None] * jnp.asarray(freq)[None, :]
        tables = jnp.stack([jnp.cos(angles), jnp.sin(angles) * jnp.asarray(sign)[None, :]])
        w_dkv_t = jnp.swapaxes(w_dkv, 1, 2)
        w_uv_t = jnp.swapaxes(w_uv, 2, 3)
        new = []
        for layer, cache in enumerate((cache0, cache1)):
            part, cache_t = attention(layer, lengths, x, tables, attn_gain, kv_gain, q_gain, jnp.swapaxes(cache, 1, 2), w_dkv_t, w_qa, w_qb, w_uk, w_uv_t, w_o)
            x = ffn(layer, ranks, tp_size, part, x, ffn_gain, w_gate, w_up, w_down)
            new.append(jnp.swapaxes(cache_t, 1, 2))
        return x, new[0], new[1]

    return jax.shard_map(local_step, mesh=mesh, in_specs=in_specs, out_specs=out_specs, check_vma=False)
```

time: 484 us -> 60 us (0.12)
  blocking collectives: 389 us -> 0 us
  Pallas kernels: 0 us -> 53.9 us
  matrix products: 43.4 us -> 0 us
  local copies, waits for them, and re-layouts: 22.5 us -> 2.65 us
  other arithmetic: 13 us -> 2.31 us
  waiting for transfers between devices: 8.27 us -> 0 us
  starting transfers between devices: 5.46 us -> 0 us
    all_gather x2 -> x0, blocking collectives: 301 us -> none  [local_step(): all_in = lax.all_gather(ffn_in, 'dp', axis=0, tiled=True)]
    psum x4 -> x0, blocking collectives: 73.2 us -> none  [the longest x2 65 us: local_step(): ffn_out = lax.psum(rank_sum, 'tp')]
    pallas_call x0 -> x4, Pallas kernels: none -> 53.9 us  [the longest x2 27.1 us: attention(): pl.pallas_call(functools.partial(attn_kernel, layer, dims), name=f'attn{l...]
    dot_general x20 -> x0, matrix products: 43.4 us -> none  [the longest x2 8.1 us: attention_local(): jnp.einsum('bht,btk->bhk', att_probs, new_cache, preferred_element_type=j...]
    all_to_all x1 -> x0, blocking collectives: 15.4 us -> none  [local_step(): received = lax.all_to_all(ffn_partial, 'dp', 0, 0, tiled=True)]
    dot_general x3 -> x0, local copies, waits for them, and re-layouts: 12.1 us -> none  [attention_local(): jnp.dot(q_low, w_qb, preferred_element_type=jnp.float32)]
    all_to_all x1 -> x0, waiting for transfers between devices: 8.27 us -> none  [local_step(): received = lax.all_to_all(ffn_partial, 'dp', 0, 0, tiled=True)]
    select_n x2 -> x0, other arithmetic: 5.48 us -> none  [attention_local(): new_cache = jnp.where(is_slot, new_entry[:, None, :], cache)]
  transfers between devices with their start and end apart: 1 -> 0, of which waited for: 1 -> 0; matrix products, arithmetic and copies ran while one was open for 1% -> 0% of each run, Pallas kernels for 0% -> 0%
where the time goes in v1:
time: 60 us; the launch traced here: 59.6 us
  Pallas kernels  53.9 us (90%)
  local copies, waits for them, and re-layouts  2.65 us (4%)
  other arithmetic  2.31 us (4%)
  between operations  0.71 us (1%)
    pallas_call x2, Pallas kernels, attention(): pl.pallas_call(functools.partial(attn_kernel, layer, dims), name=f'attn{l...  27.1 us
    pallas_call x2, Pallas kernels, ffn(): pl.pallas_call(functools.partial(ffn_kernel, layer, (ranks, tp, rows, til...  26.7 us
    unnamed x13, local copies, waits for them, and re-layouts  2.65 us

profile of v1, /device:TPU:1, one launch (start us, length us, event | category | flops | bytes accessed | tf_op | source)
XLA Modules:
  0.0 59.6 jit_solution(11579094518574964299)
XLA Ops:
  0.6 0.7 %convert_element_type.3 = f32[2]{0:T(128)S(1)} convert(s32[2]{0:T(128)} %len_ref.3) | non-fusion elementwise | flops 2 | bytes 16 | tf_op jit(solution)/shard_map/convert_element_type | solution.py:347
  1.3 1.0 %multiply_cosine_fusion = (f32[1,2,2048]{2,1,0:T(2,128)S(1)}, f32[1,2,2048]{2,1,0:T(2,128)S(1)}) fusion(f32[2048]{0:T(1024)} %constant.4.clone, f32[2]{0:T(128)S(1)} %convert_element_type.3, f32[2048]{0:T(1024)} %constant.5.clone), kind=kLoop, calls=%fused_computation.2 | loop fusion | flops 8192 | bytes 49160 | tf_op jit(solution)/shard_map/cos | solution.py:348
  2.3 0.6 %pad_maximum_fusion.tab_ref = f32[2,2,2048]{2,1,0:T(2,128)} fusion(f32[1,2,2048]{2,1,0:T(2,128)S(1)} %get-tuple-element.12, f32[1,2,2048]{2,1,0:T(2,128)S(1)} %get-tuple-element.11), kind=kLoop, calls=%fused_computation | loop fusion | flops 8192 | bytes 65536 | tf_op jit(solution)/shard_map/stack | solution.py:348
  2.9 0.0 copy-start.2
  2.9 0.0 copy-start.3
  2.9 13.5 %attn0.1 = (f32[2,2560]{1,0:T(2,128)}, bf16[2,288,4096]{2,1,0:T(8,128)(2,1)}) custom-call(s32[2]{0:T(128)} %len_ref.3, bf16[2,2560]{1,0:T(2,128)(2,1)} %x_ref.3, f32[2,2,2048]{2,1,0:T(2,128)} %pad_maximum_fusion.tab_ref, f32[2,2560]{1,0:T(2,128)} %attn_g.3, f32[2,256]{1,0:T(2,128)} %kv_g.3, f32[2,768]{1,0:T(2,128)} %q_g.3, bf16[2,288,4096]{2,1,0:T(8,128)(2,1)} %bitcast.10, ...), custom_call_target="tpu_custom_call" | custom-call | flops 200000000 | bytes 26000000 | tf_op jit(solution)/shard_map/attn0/pallas_call | solution.py:189
  16.4 0.0 copy-done.2
  16.5 0.0 copy-done.3
  16.5 0.0 copy-start.5
  16.5 0.7 %copy-done.5 = f32[2,2560]{1,0:T(2,128)S(1)} copy-done((f32[2,2560]{1,0:T(2,128)S(1)}, f32[2,2560]{1,0:T(2,128)}, u32[]{:S(2)}) %copy-start.5) | copy-done | bytes 20504
  17.2 14.8 %ffn0.1.x_ref = bf16[2,2560]{1,0:T(2,128)(2,1)S(1)} custom-call(f32[2,2560]{1,0:T(2,128)S(1)} %copy-done.5, bf16[2,2560]{1,0:T(2,128)(2,1)S(1)} %copy-done.3, f32[2,2560]{1,0:T(2,128)S(1)} %copy-done.2, bf16[2,2560,6400]{2,1,0:T(8,128)(2,1)} %w_gate.3, bf16[2,2560,6400]{2,1,0:T(8,128)(2,1)} %w_up.3, bf16[2,6400,2560]{2,1,0:T(8,128)(2,1)} %w_down.3), custom_call_target="tpu_custom_call" | custom-call | flops 200000000 | bytes 14000000 | tf_op jit(solution)/shard_map/ffn0/pallas_call | solution.py:309
  32.0 0.0 copy-start
  32.1 0.6 copy-done
  32.6 0.0 copy-start.1
  32.6 13.7 %attn1.1 = (f32[2,2560]{1,0:T(2,128)}, bf16[2,288,4096]{2,1,0:T(8,128)(2,1)}) custom-call(s32[2]{0:T(128)} %len_ref.3, bf16[2,2560]{1,0:T(2,128)(2,1)} %copy-done, f32[2,2,2048]{2,1,0:T(2,128)} %pad_maximum_fusion.tab_ref, f32[2,2560]{1,0:T(2,128)} %attn_g.3, f32[2,256]{1,0:T(2,128)} %kv_g.3, f32[2,768]{1,0:T(2,128)} %q_g.3, bf16[2,288,4096]{2,1,0:T(8,128)(2,1)} %bitcast.11, ...), custom_call_target="tpu_custom_call" | custom-call | flops 200000000 | bytes 26000000 | tf_op jit(solution)/shard_map/attn1/pallas_call | solution.py:189
  46.3 0.0 copy-done.1
  46.3 0.0 copy-start.4
  46.3 0.7 %copy-done.4 = f32[2,2560]{1,0:T(2,128)S(1)} copy-done((f32[2,2560]{1,0:T(2,128)S(1)}, f32[2,2560]{1,0:T(2,128)}, u32[]{:S(2)}) %copy-start.4) | copy-done | bytes 20504
  47.0 11.9 %ffn1.1 = bf16[2,2560]{1,0:T(2,128)(2,1)S(1)} custom-call(f32[2,2560]{1,0:T(2,128)S(1)} %copy-done.4, bf16[2,2560]{1,0:T(2,128)(2,1)S(1)} %copy-done.1, f32[2,2560]{1,0:T(2,128)S(1)} %copy-done.2, bf16[2,2560,6400]{2,1,0:T(8,128)(2,1)} %w_gate.3, bf16[2,2560,6400]{2,1,0:T(8,128)(2,1)} %w_up.3, bf16[2,6400,2560]{2,1,0:T(8,128)(2,1)} %w_down.3), custom_call_target="tpu_custom_call" | custom-call | flops 200000000 | bytes 14000000 | tf_op jit(solution)/shard_map/ffn1/pallas_call | solution.py:309
  59.0 0.6 %copy.23 = bf16[2,2560]{1,0:T(2,128)(2,1)} copy(bf16[2,2560]{1,0:T(2,128)(2,1)S(1)} %ffn1.1) | data formatting | bytes 20480
Async XLA Ops:
  2.9 13.5 %copy-start.2 = (f32[2,2560]{1,0:T(2,128)S(1)}, f32[2,2560]{1,0:T(2,128)}, u32[]{:S(2)}) copy-start(f32[2,2560]{1,0:T(2,128)} %ffn_g.3) | copy-start | bytes 61444
  2.9 13.5 %copy-start.3 = (bf16[2,2560]{1,0:T(2,128)(2,1)S(1)}, bf16[2,2560]{1,0:T(2,128)(2,1)}, u32[]{:S(2)}) copy-start(bf16[2,2560]{1,0:T(2,128)(2,1)} %x_ref.3) | copy-start | bytes 30724
  16.5 0.7 %copy-start.5 = (f32[2,2560]{1,0:T(2,128)S(1)}, f32[2,2560]{1,0:T(2,128)}, u32[]{:S(2)}) copy-start(f32[2,2560]{1,0:T(2,128)} %get-tuple-element.7.part_ref) | copy-start | bytes 61444
  32.0 0.6 %copy-start = (bf16[2,2560]{1,0:T(2,128)(2,1)}, bf16[2,2560]{1,0:T(2,128)(2,1)S(1)}, u32[]{:S(2)}) copy-start(bf16[2,2560]{1,0:T(2,128)(2,1)S(1)} %ffn0.1.x_ref) | copy-start | bytes 30724
  32.6 13.7 %copy-start.1 = (bf16[2,2560]{1,0:T(2,128)(2,1)S(1)}, bf16[2,2560]{1,0:T(2,128)(2,1)}, u32[]{:S(2)}) copy-start(bf16[2,2560]{1,0:T(2,128)(2,1)} %copy-done) | copy-start | bytes 30724
  46.3 0.7 %copy-start.4 = (f32[2,2560]{1,0:T(2,128)S(1)}, f32[2,2560]{1,0:T(2,128)}, u32[]{:S(2)}) copy-start(f32[2,2560]{1,0:T(2,128)} %get-tuple-element.8.part_ref) | copy-start | bytes 61444

commit v2 on v0

v2 whole, which is shorter than its diff:
```python
import functools

import jax
import jax.numpy as jnp
import numpy as np
from jax import lax
from jax.experimental import pallas as pl
from jax.experimental.pallas import tpu as pltpu
from jax.sharding import PartitionSpec as P

MESH = pl.DeviceIdType.MESH
NORM_EPS = 1e-6
ROPE_BASE = 10000.0
HEAD_PAD = 24
LANES = 128
CHUNK = 1024
OUT_CHUNK = 512
SIDE = 4
VMEM_SPEC = pl.BlockSpec(memory_space=pltpu.VMEM)
SMEM_SPEC = pl.BlockSpec(memory_space=pltpu.SMEM)
HBM_SPEC = pl.BlockSpec(memory_space=pltpu.HBM)
NT = (((1,), (1,)), ((), ()))
F32 = jnp.float32
BF16 = jnp.bfloat16


def dot(a, b):
    return jnp.dot(a, b, preferred_element_type=F32)


def dot_nt(a, b):
    return lax.dot_general(a, b, NT, preferred_element_type=F32)


def rms(values, gain):
    inv = lax.rsqrt(jnp.mean(values * values, axis=-1, keepdims=True) + NORM_EPS)
    return (values * inv * gain).astype(BF16)


def rope_lanes(head_width, nope, rope, period):
    half = rope // 2
    turns = ROPE_BASE ** (-2.0 * np.arange(half) / rope) / (2.0 * np.pi)
    freq = np.zeros(period + LANES)
    sign = np.zeros(period + LANES)
    for s in [h * head_width + nope for h in range(period // head_width)] + [period]:
        freq[s:s + half] = turns
        freq[s + half:s + rope] = turns
        sign[s:s + half] = -1.0
        sign[s + half:s + rope] = 1.0
    mant, expo = np.frexp(freq)
    high = np.ldexp(np.floor(mant * 2.0 ** 12), expo - 12)
    table = np.zeros((8, period + LANES), np.float32)
    table[0], table[1], table[2] = high, freq - high, sign
    return table


def series(x, terms):
    out = jnp.full(x.shape, terms[-1], F32)
    for t in terms[-2::-1]:
        out = out * x + t
    return out


def cos_sin(turns):
    x = turns * np.float32(np.pi)
    x2 = x * x
    fact = np.cumprod([1.0] + list(range(1, 18)))
    s = x * series(x2, [np.float32((-1.0) ** i / fact[2 * i + 1]) for i in range(8)])
    c = series(x2, [np.float32((-1.0) ** i / fact[2 * i]) for i in range(9)])
    return 1.0 - 2.0 * s * s, 2.0 * s * c


def step_kernel(dims, len_ref, lane_ref, x_ref, attn_g, kv_g, q_g, ffn_g, cache0, cache1, w_dkv, w_qa, w_qb, w_uk, w_uv, w_o, w_gate, w_up, w_down,
                x_out, entry_out, c_out0, c_out1,
                dkv_b, qa_b, qb_b, uk_b, uv_b, o_b, gate_b, up_b, down_b, s_b, mine_b, part_b, mid_b, all_b, send_b, sum_b,
                a_sems, f_sems, ps, pr, ms, mr, rs, rr):
    layers, rows, heads, nope, rope, lat, slots, tiles_all, tiles, ranks, tp, period = dims
    half = rope // 2
    hw = nope + rope
    width = heads * hw
    entry_w = lat + rope
    members = ranks * tp
    caches = (cache0, cache1)
    cache_b = (c_out0, c_out1)

    c = lax.axis_index("tp")
    d = lax.axis_index("dp")
    xx = lax.rem(d, SIDE)
    yy = lax.rem(d // SIDE, SIDE)
    pos = lax.rem(yy, 2) * 2 + lax.rem(xx, 2)
    corner = d - lax.rem(yy, 2) * SIDE - lax.rem(xx, 2)
    me = pos * tp + c

    def dp_of(q):
        return corner + (q // 2) * SIDE + lax.rem(q, 2)

    start = tiles_all * me // members
    count = tiles_all * (me + 1) // members - start
    base_tile = jnp.minimum(start, tiles_all - tiles)
    skip = start - base_tile
    first = pl.multiple_of(base_tile * LANES, LANES)

    qa_rows = w_qa.shape[1] // 2
    qb_rows = w_qb.shape[1] // 2
    o_rows = w_o.shape[1] // 4

    def attn_loads(layer):
        pairs = [("dkv", w_dkv.at[layer], dkv_b)]
        for i in range(2):
            cut = pl.ds(i * qa_rows, qa_rows)
            pairs.append((f"qa{i}", w_qa.at[layer, cut], qa_b.at[cut]))
        for i in range(2):
            cut = pl.ds(i * qb_rows, qb_rows)
            pairs.append((f"qb{i}", w_qb.at[layer, cut], qb_b.at[cut]))
        pairs.append(("uk", w_uk.at[layer], uk_b.at[:, pl.ds(0, nope), pl.ds(0, lat)]))
        for r in range(rows):
            pairs.append((f"c{r}", caches[layer].at[r], cache_b[layer].at[r]))
        pairs.append(("uv", w_uv.at[layer], uv_b))
        for i in range(4):
            cut = pl.ds(i * o_rows, o_rows)
            pairs.append((f"o{i}", w_o.at[layer, cut], o_b.at[cut]))
        loads = {name: pltpu.make_async_copy(a, b, a_sems.at[i]) for i, (name, a, b) in enumerate(pairs)}
        for load in loads.values():
            load.start()
        return loads

    def ffn_loads(layer):
        loads = [
            pltpu.make_async_copy(w_gate.at[layer, :, pl.ds(first, tiles * LANES)], gate_b, f_sems.at[0]),
            pltpu.make_async_copy(w_up.at[layer, :, pl.ds(first, tiles * LANES)], up_b, f_sems.at[1]),
            pltpu.make_async_copy(w_down.at[layer, pl.ds(first, tiles * LANES)], down_b, f_sems.at[2]),
        ]
        for load in loads:
            load.start()
        return loads

    a_loads = attn_loads(0)
    f_loads = ffn_loads(0)

    def peer(k):
        other = lax.rem(me + k, members)
        return other // tp, lax.rem(other, tp)

    barrier = pltpu.get_barrier_semaphore()
    for k in range(1, members):
        q, t = peer(k)
        pl.semaphore_signal(barrier, inc=1, device_id={"tp": t, "dp": dp_of(q)}, device_id_type=MESH)

    uk_b[:, nope:, :lat] = jnp.zeros((heads, rope, lat), BF16)
    sub = lax.broadcasted_iota(jnp.int32, (heads, hw, LANES), 1)
    lan = lax.broadcasted_iota(jnp.int32, (heads, hw, LANES), 2)
    uk_b[:, :, lat:] = jnp.where(sub == lan + nope, 1.0, 0.0).astype(BF16)
    entry_out[...] = jnp.zeros(entry_out.shape, F32)

    shape = (rows, period + LANES)
    row_id = lax.broadcasted_iota(jnp.int32, shape, 0)
    where_at = jnp.full(shape, len_ref[0].astype(F32))
    for r in range(1, rows):
        where_at = jnp.where(row_id == r, len_ref[r].astype(F32), where_at)
    turns = where_at * lane_ref[0:1, :]
    turns = (turns - jnp.floor(turns + 0.5)) + where_at * lane_ref[1:2, :]
    turns = turns - jnp.floor(turns + 0.5)
    cos_t, sin_t = cos_sin(turns)
    sin_t = sin_t * lane_ref[2:3, :]
    repeat = width // period
    cos_q = jnp.concatenate([cos_t[:, :period]] * repeat, axis=1)
    sin_q = jnp.concatenate([sin_t[:, :period]] * repeat, axis=1)
    cos_k, sin_k = cos_t[:, period:], sin_t[:, period:]
    sign_q = jnp.concatenate([jnp.broadcast_to(lane_ref[2:3, :period], (rows, period))] * repeat, axis=1)
    sign_k = jnp.broadcast_to(lane_ref[2:3, period:], (rows, LANES))

    spread_shape = (HEAD_PAD, width)
    head = lax.broadcasted_iota(jnp.int32, spread_shape, 0) * hw
    lane = lax.broadcasted_iota(jnp.int32, spread_shape, 1)
    spread_own = (lane >= head) & (lane < head + hw)
    v_dim = w_uv.shape[2]
    pick_shape = (HEAD_PAD, heads * v_dim)
    head = lax.broadcasted_iota(jnp.int32, pick_shape, 0) * v_dim
    lane = lax.broadcasted_iota(jnp.int32, pick_shape, 1)
    pick_own = (lane >= head) & (lane < head + v_dim)
    scale = hw ** -0.5
    x = x_ref[...].astype(F32)
    sends = []

    for layer in range(layers):
        cache = cache_b[layer]
        h = rms(x, attn_g[layer:layer + 1, :])
        a_loads["dkv"].wait()
        kv = dot_nt(h, dkv_b[...])
        k_lat = rms(kv[:, :lat], kv_g[layer:layer + 1, :])
        k_raw = jnp.concatenate([kv[:, lat:], jnp.zeros((rows, LANES - rope), F32)], axis=1)
        k_other = jnp.where(sign_k < 0, pltpu.roll(k_raw, LANES - half, 1), pltpu.roll(k_raw, half, 1))
        k_rot = (k_raw * cos_k + k_other * sin_k).astype(BF16)
        entry = jnp.concatenate([k_lat.astype(F32), k_rot.astype(F32)], axis=1)
        entry_out[layer * rows:(layer + 1) * rows, :] = entry

        qa = jnp.zeros((rows, w_qa.shape[2]), F32)
        for i in range(2):
            a_loads[f"qa{i}"].wait()
            qa += dot(h[:, i * qa_rows:(i + 1) * qa_rows], qa_b[pl.ds(i * qa_rows, qa_rows)])
        q_low = rms(qa, q_g[layer:layer + 1, :])
        q = jnp.zeros((rows, width), F32)
        for i in range(2):
            a_loads[f"qb{i}"].wait()
            q += dot(q_low[:, i * qb_rows:(i + 1) * qb_rows], qb_b[pl.ds(i * qb_rows, qb_rows)])
        q_other = jnp.where(sign_q < 0, pltpu.roll(q, width - half, 1), pltpu.roll(q, half, 1))
        q = q * cos_q + q_other * sin_q
        spread = jnp.concatenate([jnp.where(spread_own, jnp.broadcast_to(q[r:r + 1], spread_shape), 0.0) for r in range(rows)], axis=0).astype(BF16)
        a_loads["uk"].wait()
        query = dot(spread, uk_b[...].reshape(width, lat + LANES))

        o_lat = []
        for r in range(rows):
            a_loads[f"c{r}"].wait()
            length = len_ref[r]
            q_r = query[r * HEAD_PAD:(r + 1) * HEAD_PAD].astype(BF16)
            s_new = jnp.sum(q_r.astype(F32) * entry[r:r + 1], axis=1, keepdims=True) * scale
            top = s_new
            for k in range(slots // CHUNK):
                cols = pl.ds(k * CHUNK, CHUNK)
                s = dot(q_r[:, :lat], cache[r, pl.ds(0, lat), cols]) + dot(q_r[:, lat:entry_w], cache[r, pl.ds(lat, rope), cols])
                slot = lax.broadcasted_iota(jnp.int32, s.shape, 1) + k * CHUNK
                s = jnp.where(slot < length, s * scale, -1e30)
                s_b[r, :, cols] = s
                top = jnp.maximum(top, jnp.max(s, axis=1, keepdims=True))
            e_new = jnp.exp(s_new - top)
            total = e_new
            for k in range(slots // CHUNK):
                cols = pl.ds(k * CHUNK, CHUNK)
                e = jnp.exp(s_b[r, :, cols] - top)
                s_b[r, :, cols] = e
                total += jnp.sum(e, axis=1, keepdims=True)
            inv = 1.0 / total
            acc = (e_new * inv).astype(BF16).astype(F32) * entry[r:r + 1, :lat]
            for k in range(slots // CHUNK):
                cols = pl.ds(k * CHUNK, CHUNK)
                p = (s_b[r, :, cols] * inv).astype(BF16)
                acc += dot_nt(p, cache[r, pl.ds(0, lat), cols])
            o_lat.append(acc)
        o_lat = jnp.concatenate(o_lat, axis=0).astype(BF16)
        a_loads["uv"].wait()
        wide = dot_nt(o_lat, uv_b[...].reshape(heads * v_dim, lat))
        o = [jnp.sum(jnp.where(pick_own, wide[r * HEAD_PAD:(r + 1) * HEAD_PAD], 0.0), axis=0, keepdims=True) for r in range(rows)]
        o = jnp.concatenate(o, axis=0).astype(BF16)
        part = x * jnp.where(c == 0, 1.0, 0.0)
        for i in range(4):
            a_loads[f"o{i}"].wait()
            part += dot(o[:, i * o_rows:(i + 1) * o_rows], o_b[pl.ds(i * o_rows, o_rows)])

        mine_b[layer] = part
        if layer == 0:
            pl.semaphore_wait(barrier, members - 1)
        swap = pltpu.make_async_remote_copy(
            src_ref=mine_b.at[layer], dst_ref=part_b.at[layer], send_sem=ps.at[layer], recv_sem=pr.at[layer],
            device_id={"tp": 1 - c, "dp": d}, device_id_type=MESH)
        swap.start()
        if layer + 1 < layers:
            a_loads = attn_loads(layer + 1)
        swap.wait_recv()
        x_mid = (part + part_b[layer]).astype(BF16)
        mid_b[layer, pos] = x_mid

        gathers = []
        for k in range(1, ranks):
            q = lax.rem(pos + k, ranks)
            for t in range(tp):
                gathers.append(pltpu.make_async_remote_copy(
                    src_ref=mid_b.at[layer, pos], dst_ref=mid_b.at[layer, pos], send_sem=ms.at[layer, k - 1, t], recv_sem=mr.at[layer, k - 1],
                    device_id={"tp": t, "dp": dp_of(q)}, device_id_type=MESH))

        @pl.when(c == tp - 1)
        def _():
            for copy in gathers:
                copy.start()
        for k in range(ranks - 1):
            gathers[k * tp].wait_recv()

        for q in range(ranks):
            all_b[q * rows:(q + 1) * rows, :] = mid_b[layer, q].astype(F32)
        g = rms(all_b[...], ffn_g[layer:layer + 1, :])
        f_loads[0].wait()
        a = dot(g, gate_b[...])
        f_loads[1].wait()
        b = dot(g, up_b[...])
        lane = lax.broadcasted_iota(jnp.int32, a.shape, 1)
        kept = (lane >= skip * LANES) & (lane < (skip + count) * LANES)
        u = jnp.where(kept, a * jax.nn.sigmoid(a) * b, 0.0).astype(BF16)
        f_loads[2].wait()
        partial = dot(u, down_b[...])
        for q in range(ranks):
            send_b[layer, q] = partial[q * rows:(q + 1) * rows].astype(BF16)
        sum_b[layer, me] = send_b[layer, pos]

        returns = []
        for k in range(1, members):
            q, t = peer(k)
            returns.append(pltpu.make_async_remote_copy(
                src_ref=send_b.at[layer, q], dst_ref=sum_b.at[layer, me], send_sem=rs.at[layer, k - 1], recv_sem=rr.at[layer, k - 1],
                device_id={"tp": t, "dp": dp_of(q)}, device_id_type=MESH))
        for copy in returns:
            copy.start()
        if layer + 1 < layers:
            f_loads = ffn_loads(layer + 1)
        for copy in returns:
            copy.wait_recv()
        total = sum_b[layer, 0].astype(F32)
        for j in range(1, members):
            total = total + sum_b[layer, j].astype(F32)
        x_new = (x_mid.astype(F32) + total).astype(BF16)
        x = x_new.astype(F32)
        sends.append((swap, gathers, returns))

    x_out[...] = x_new
    for swap, gathers, returns in sends:
        swap.wait_send()
        for copy in returns:
            copy.wait_send()

        @pl.when(c == tp - 1)
        def _():
            for copy in gathers:
                copy.wait_send()


def write_kernel(dims, len_ref, x_ref, entry_ref, c0, c1, x_out, out0, out1, patch_b, sems):
    layers, rows, entry_w, slots = dims
    x_out[...] = x_ref[...]
    entry_t = entry_ref[...].T[:entry_w]
    caches, outs = (c0, c1), (out0, out1)
    for layer in range(layers):
        for r in range(rows):
            length = len_ref[r]
            home = length // OUT_CHUNK
            for k in range(slots // OUT_CHUNK):
                cols = pl.ds(k * OUT_CHUNK, OUT_CHUNK)

                @pl.when(home != k)
                def _():
                    pltpu.make_async_copy(caches[layer].at[r, :, cols], outs[layer].at[r, :, cols], sems.at[layer, r]).start()
    for layer in range(layers):
        for r in range(rows):
            length = len_ref[r]
            base = pl.multiple_of(length // OUT_CHUNK * OUT_CHUNK, OUT_CHUNK)
            tile = caches[layer][r, :, pl.ds(base, OUT_CHUNK)].astype(F32)
            lane = lax.broadcasted_iota(jnp.int32, tile.shape, 1)
            column = entry_t[:, layer * rows + r:layer * rows + r + 1]
            patch_b[layer, r] = jnp.where(lane == length - base, jnp.broadcast_to(column, tile.shape), tile).astype(BF16)
            pltpu.make_async_copy(patch_b.at[layer, r], outs[layer].at[r, :, pl.ds(base, OUT_CHUNK)], sems.at[layer, r]).start()
    for layer in range(layers):
        for r in range(rows):
            pltpu.make_async_copy(caches[layer].at[r], outs[layer].at[r], sems.at[layer, r]).wait()


def solution(mesh):
    tp_size = mesh.shape['tp']
    ranks = 4
    row_spec = P(('rep', 'dp'), None)
    cache_spec = P(('rep', 'dp'), None, None)
    in_specs = (row_spec, P(('rep', 'dp')), cache_spec, cache_spec, P(), P(), P(), P(), P(), P(), P(None, None, 'tp'), P(None, 'tp', None, None), P(None, 'tp', None, None), P(None, 'tp', None), P(), P(), P())
    out_specs = (row_spec, cache_spec, cache_spec)

    def local_step(x, lengths, cache0, cache1, attn_gain, kv_gain, q_gain, ffn_gain, w_dkv, w_qa, w_qb, w_uk, w_uv, w_o, w_gate, w_up, w_down):
        rows, model = x.shape
        layers, heads, nope, lat = w_uk.shape
        slots = cache0.shape[1]
        rope = cache0.shape[2] - lat
        hw = nope + rope
        period = int(np.lcm(hw, LANES))
        tiles_all = w_gate.shape[2] // LANES
        members = ranks * tp_size
        tiles = -(-tiles_all // members)
        lanes = jnp.asarray(rope_lanes(hw, nope, rope, period))
        c0, c1 = jnp.swapaxes(cache0, 1, 2), jnp.swapaxes(cache1, 1, 2)
        w_dkv_t = jnp.swapaxes(w_dkv, 1, 2)
        w_uv_t = jnp.swapaxes(w_uv, 2, 3)
        dims = (layers, rows, heads, nope, rope, lat, slots, tiles_all, tiles, ranks, tp_size, period)
        dma = pltpu.SemaphoreType.DMA
        x_new, entries, held0, held1 = pl.pallas_call(
            functools.partial(step_kernel, dims),
            name="step",
            out_shape=(pltpu.VMEM((rows, model), BF16), pltpu.VMEM((8, lat + LANES), F32), pltpu.VMEM(c0.shape, BF16), pltpu.VMEM(c1.shape, BF16)),
            in_specs=[SMEM_SPEC] + [VMEM_SPEC] * 6 + [HBM_SPEC] * 11,
            out_specs=(VMEM_SPEC, VMEM_SPEC, VMEM_SPEC, VMEM_SPEC),
            scratch_shapes=[
                pltpu.VMEM(w_dkv_t.shape[1:], BF16),
                pltpu.VMEM(w_qa.shape[1:], BF16),
                pltpu.VMEM(w_qb.shape[1:], BF16),
                pltpu.VMEM((heads, hw, lat + LANES), BF16),
                pltpu.VMEM(w_uv_t.shape[1:], BF16),
                pltpu.VMEM(w_o.shape[1:], BF16),
                pltpu.VMEM((model, tiles * LANES), BF16),
                pltpu.VMEM((model, tiles * LANES), BF16),
                pltpu.VMEM((tiles * LANES, model), BF16),
                pltpu.VMEM((rows, HEAD_PAD, slots), F32),
                pltpu.VMEM((layers, rows, model), F32),
                pltpu.VMEM((layers, rows, model), F32),
                pltpu.VMEM((layers, ranks, rows, model), BF16),
                pltpu.VMEM((ranks * rows, model), F32),
                pltpu.VMEM((layers, ranks, rows, model), BF16),
                pltpu.VMEM((layers, members, rows, model), BF16),
                dma((13,)),
                dma((3,)),
                dma((layers,)),
                dma((layers,)),
                dma((layers, ranks - 1, tp_size)),
                dma((layers, ranks - 1)),
                dma((layers, members - 1)),
                dma((layers, members - 1)),
            ],
            compiler_params=pltpu.CompilerParams(collective_id=0, has_side_effects=True, vmem_limit_bytes=46 * 2 ** 20),
            cost_estimate=pl.CostEstimate(flops=10 ** 9, bytes_accessed=70 * 10 ** 6, transcendentals=4 * 10 ** 5),
        )(lengths, lanes, x, attn_gain, kv_gain, q_gain, ffn_gain, c0, c1, w_dkv_t, w_qa, w_qb, w_uk, w_uv_t, w_o, w_gate, w_up, w_down)
        x_new, new0, new1 = pl.pallas_call(
            functools.partial(write_kernel, (layers, rows, lat + rope, slots)),
            name="write",
            out_shape=(jax.ShapeDtypeStruct(x.shape, BF16), jax.ShapeDtypeStruct(c0.shape, BF16), jax.ShapeDtypeStruct(c1.shape, BF16)),
            in_specs=[SMEM_SPEC, VMEM_SPEC, VMEM_SPEC, VMEM_SPEC, VMEM_SPEC],
            out_specs=(VMEM_SPEC, HBM_SPEC, HBM_SPEC),
            scratch_shapes=[pltpu.VMEM((layers, rows, lat + rope, OUT_CHUNK), BF16), dma((layers, rows))],
            compiler_params=pltpu.CompilerParams(vmem_limit_bytes=24 * 2 ** 20),
            cost_estimate=pl.CostEstimate(flops=10 ** 6, bytes_accessed=20 * 10 ** 6, transcendentals=0),
        )(lengths, x_new, entries, held0, held1)
        return x_new, jnp.swapaxes(new0, 1, 2), jnp.swapaxes(new1, 1, 2)

    return jax.shard_map(local_step, mesh=mesh, in_specs=in_specs, out_specs=out_specs, check_vma=False)
```

time: 484 us -> 49.9 us (0.10)
  blocking collectives: 389 us -> 0 us
  Pallas kernels: 0 us -> 49.1 us
  matrix products: 43.4 us -> 0 us
  local copies, waits for them, and re-layouts: 22.5 us -> 0.01 us
  other arithmetic: 13 us -> 0 us
  waiting for transfers between devices: 8.27 us -> 0 us
  starting transfers between devices: 5.46 us -> 0 us
    all_gather x2 -> x0, blocking collectives: 301 us -> none  [local_step(): all_in = lax.all_gather(ffn_in, 'dp', axis=0, tiled=True)]
    psum x4 -> x0, blocking collectives: 73.2 us -> none  [the longest x2 65 us: local_step(): ffn_out = lax.psum(rank_sum, 'tp')]
    pallas_call x0 -> x2, Pallas kernels: none -> 49.1 us  [the longest x1 44.2 us: local_step(): pl.pallas_call(functools.partial(step_kernel, dims), name='step', out_sha...]
    dot_general x20 -> x0, matrix products: 43.4 us -> none  [the longest x2 8.1 us: attention_local(): jnp.einsum('bht,btk->bhk', att_probs, new_cache, preferred_element_type=j...]
    all_to_all x1 -> x0, blocking collectives: 15.4 us -> none  [local_step(): received = lax.all_to_all(ffn_partial, 'dp', 0, 0, tiled=True)]
    dot_general x3 -> x0, local copies, waits for them, and re-layouts: 12.1 us -> none  [attention_local(): jnp.dot(q_low, w_qb, preferred_element_type=jnp.float32)]
    all_to_all x1 -> x0, waiting for transfers between devices: 8.27 us -> none  [local_step(): received = lax.all_to_all(ffn_partial, 'dp', 0, 0, tiled=True)]
    unnamed x24 -> x2, local copies, waits for them, and re-layouts: 6.33 us -> 0.01 us
  transfers between devices with their start and end apart: 1 -> 0, of which waited for: 1 -> 0; matrix products, arithmetic and copies ran while one was open for 1% -> 0% of each run, Pallas kernels for 0% -> 0%
where the time goes in v2:
time: 49.9 us; the launch traced here: 49.7 us
  Pallas kernels  49.1 us (98%)
  between operations  0.66 us (1%)
    pallas_call x1, Pallas kernels, local_step(): pl.pallas_call(functools.partial(step_kernel, dims), name='step', out_sha...  44.2 us
    pallas_call x1, Pallas kernels, local_step(): pl.pallas_call(functools.partial(write_kernel, (layers, rows, lat + rope,...  4.86 us

profile of v2, /device:TPU:1, one launch (start us, length us, event | category | flops | bytes accessed | tf_op | source)
XLA Modules:
  0.0 49.7 jit_solution(3259141328320742322)
XLA Ops:
  0.6 0.0 copy-start
  0.6 44.2 %step.1 = (bf16[2,2560]{1,0:T(2,128)(2,1)S(1)}, f32[8,384]{1,0:T(8,128)S(1)}, bf16[2,288,4096]{2,1,0:T(8,128)(2,1)S(1)}, bf16[2,288,4096]{2,1,0:T(8,128)(2,1)S(1)}) custom-call(s32[2]{0:T(128)} %len_ref.3, f32[8,512]{1,0:T(8,128)} %constant.2.clone.lane_ref, bf16[2,2560]{1,0:T(2,128)(2,1)} %x_ref.1, f32[2,2560]{1,0:T(2,128)} %attn_g.1, f32[2,256]{1,0:T(2,128)} %kv_g.1, ...), custom_call_target="tpu_custom_call" | custom-call | flops 1000000000 | bytes 70000000 | tf_op jit(solution)/shard_map/step/pallas_call | solution.py:378
  44.9 0.0 copy-done
  44.9 4.9 %write.1 = (bf16[2,2560]{1,0:T(2,128)(2,1)}, bf16[2,288,4096]{2,1,0:T(8,128)(2,1)}, bf16[2,288,4096]{2,1,0:T(8,128)(2,1)}) custom-call(s32[2]{0:T(128)S(1)} %copy-done, bf16[2,2560]{1,0:T(2,128)(2,1)S(1)} %get-tuple-element.10.x_ref, f32[8,384]{1,0:T(8,128)S(1)} %get-tuple-element.11.entry_ref, bf16[2,288,4096]{2,1,0:T(8,128)(2,1)S(1)} %get-tuple-element.12.c0, ...), custom_call_target="tpu_custom_call" | custom-call | flops 1000000 | bytes 20000000 | tf_op jit(solution)/shard_map/write/pallas_call | solution.py:413
Async XLA Ops:
  0.6 44.2 %copy-start = (s32[2]{0:T(128)S(1)}, s32[2]{0:T(128)}, u32[]{:S(2)}) copy-start(s32[2]{0:T(128)} %len_ref.3) | copy-start | bytes 28

commit v3 on v2

--- a/solution.py
+++ b/solution.py
@@ -13,6 +13,7 @@
 ROPE_BASE = 10000.0
 HEAD_PAD = 24
 LANES = 128
+PASS = 256
 CHUNK = 1024
 OUT_CHUNK = 512
 SIDE = 4
@@ -54,6 +55,12 @@
     return table
 
 
+def cuts(size, count):
+    step = size // count // PASS * PASS
+    starts = [i * step for i in range(count)]
+    return [(a, b - a) for a, b in zip(starts, starts[1:] + [size])]
+
+
 def series(x, terms):
     out = jnp.full(x.shape, terms[-1], F32)
     for t in terms[-2::-1]:
@@ -101,23 +108,20 @@
     first = pl.multiple_of(base_tile * LANES, LANES)
 
     qa_rows = w_qa.shape[1] // 2
-    qb_rows = w_qb.shape[1] // 2
-    o_rows = w_o.shape[1] // 4
+    o_cuts = cuts(w_o.shape[1], 2)
 
     def attn_loads(layer):
         pairs = [("dkv", w_dkv.at[layer], dkv_b)]
         for i in range(2):
             cut = pl.ds(i * qa_rows, qa_rows)
             pairs.append((f"qa{i}", w_qa.at[layer, cut], qa_b.at[cut]))
-        for i in range(2):
-            cut = pl.ds(i * qb_rows, qb_rows)
-            pairs.append((f"qb{i}", w_qb.at[layer, cut], qb_b.at[cut]))
+        pairs.append(("qb", w_qb.at[layer], qb_b))
         pairs.append(("uk", w_uk.at[layer], uk_b.at[:, pl.ds(0, nope), pl.ds(0, lat)]))
         for r in range(rows):
             pairs.append((f"c{r}", caches[layer].at[r], cache_b[layer].at[r]))
         pairs.append(("uv", w_uv.at[layer], uv_b))
-        for i in range(4):
-            cut = pl.ds(i * o_rows, o_rows)
+        for i, (at, size) in enumerate(o_cuts):
+            cut = pl.ds(at, size)
             pairs.append((f"o{i}", w_o.at[layer, cut], o_b.at[cut]))
         loads = {name: pltpu.make_async_copy(a, b, a_sems.at[i]) for i, (name, a, b) in enumerate(pairs)}
         for load in loads.values():
@@ -199,35 +203,42 @@
             a_loads[f"qa{i}"].wait()
             qa += dot(h[:, i * qa_rows:(i + 1) * qa_rows], qa_b[pl.ds(i * qa_rows, qa_rows)])
         q_low = rms(qa, q_g[layer:layer + 1, :])
-        q = jnp.zeros((rows, width), F32)
-        for i in range(2):
-            a_loads[f"qb{i}"].wait()
-            q += dot(q_low[:, i * qb_rows:(i + 1) * qb_rows], qb_b[pl.ds(i * qb_rows, qb_rows)])
+        a_loads["qb"].wait()
+        q = dot(q_low, qb_b[...])
         q_other = jnp.where(sign_q < 0, pltpu.roll(q, width - half, 1), pltpu.roll(q, half, 1))
         q = q * cos_q + q_other * sin_q
         spread = jnp.concatenate([jnp.where(spread_own, jnp.broadcast_to(q[r:r + 1], spread_shape), 0.0) for r in range(rows)], axis=0).astype(BF16)
         a_loads["uk"].wait()
         query = dot(spread, uk_b[...].reshape(width, lat + LANES))
 
+        tail = query[:, lat:]
+        group = lax.broadcasted_iota(jnp.int32, tail.shape, 0)
+        rotary = tail
+        for r in range(1, rows):
+            rotary = jnp.where(group >= r * HEAD_PAD, pltpu.roll(tail, r * rope, 1), rotary)
+        rotary = rotary[:, :rows * rope].astype(BF16)
+        q_rows = [query[r * HEAD_PAD:(r + 1) * HEAD_PAD].astype(BF16) for r in range(rows)]
+        s_new = [jnp.sum(q_rows[r].astype(F32) * entry[r:r + 1], axis=1, keepdims=True) * scale for r in range(rows)]
+        top = list(s_new)
+        for r in range(rows):
+            a_loads[f"c{r}"].wait()
+        for k in range(slots // CHUNK):
+            cols = pl.ds(k * CHUNK, CHUNK)
+            stacked = jnp.concatenate([cache[r, pl.ds(lat, rope), cols] for r in range(rows)], axis=0)
+            s_rot = dot(rotary, stacked)
+            for r in range(rows):
+                s = dot(q_rows[r][:, :lat], cache[r, pl.ds(0, lat), cols]) + s_rot[r * HEAD_PAD:(r + 1) * HEAD_PAD]
+                slot = lax.broadcasted_iota(jnp.int32, s.shape, 1) + k * CHUNK
+                s = jnp.where(slot < len_ref[r], s * scale, -1e30)
+                s_b[r, :, cols] = s
+                top[r] = jnp.maximum(top[r], jnp.max(s, axis=1, keepdims=True))
         o_lat = []
         for r in range(rows):
-            a_loads[f"c{r}"].wait()
-            length = len_ref[r]
-            q_r = query[r * HEAD_PAD:(r + 1) * HEAD_PAD].astype(BF16)
-            s_new = jnp.sum(q_r.astype(F32) * entry[r:r + 1], axis=1, keepdims=True) * scale
-            top = s_new
-            for k in range(slots // CHUNK):
-                cols = pl.ds(k * CHUNK, CHUNK)
-                s = dot(q_r[:, :lat], cache[r, pl.ds(0, lat), cols]) + dot(q_r[:, lat:entry_w], cache[r, pl.ds(lat, rope), cols])
-                slot = lax.broadcasted_iota(jnp.int32, s.shape, 1) + k * CHUNK
-                s = jnp.where(slot < length, s * scale, -1e30)
-                s_b[r, :, cols] = s
-                top = jnp.maximum(top, jnp.max(s, axis=1, keepdims=True))
-            e_new = jnp.exp(s_new - top)
+            e_new = jnp.exp(s_new[r] - top[r])
             total = e_new
             for k in range(slots // CHUNK):
                 cols = pl.ds(k * CHUNK, CHUNK)
-                e = jnp.exp(s_b[r, :, cols] - top)
+                e = jnp.exp(s_b[r, :, cols] - top[r])
                 s_b[r, :, cols] = e
                 total += jnp.sum(e, axis=1, keepdims=True)
             inv = 1.0 / total
@@ -243,9 +254,9 @@
         o = [jnp.sum(jnp.where(pick_own, wide[r * HEAD_PAD:(r + 1) * HEAD_PAD], 0.0), axis=0, keepdims=True) for r in range(rows)]
         o = jnp.concatenate(o, axis=0).astype(BF16)
         part = x * jnp.where(c == 0, 1.0, 0.0)
-        for i in range(4):
+        for i, (at, size) in enumerate(o_cuts):
             a_loads[f"o{i}"].wait()
-            part += dot(o[:, i * o_rows:(i + 1) * o_rows], o_b[pl.ds(i * o_rows, o_rows)])
+            part += dot(o[:, at:at + size], o_b[pl.ds(at, size)])
 
         mine_b[layer] = part
         if layer == 0:
@@ -279,9 +290,14 @@
             all_b[q * rows:(q + 1) * rows, :] = mid_b[layer, q].astype(F32)
         g = rms(all_b[...], ffn_g[layer:layer + 1, :])
         f_loads[0].wait()
-        a = dot(g, gate_b[...])
+        whole = tiles * LANES // PASS * PASS
+        a = dot(g, gate_b[:, :whole])
         f_loads[1].wait()
-        b = dot(g, up_b[...])
+        b = dot(g, up_b[:, :whole])
+        if whole < tiles * LANES:
+            both = dot(g, jnp.concatenate([gate_b[:, whole:], up_b[:, whole:]], axis=1))
+            a = jnp.concatenate([a, both[:, :LANES]], axis=1)
+            b = jnp.concatenate([b, both[:, LANES:]], axis=1)
         lane = lax.broadcasted_iota(jnp.int32, a.shape, 1)
         kept = (lane >= skip * LANES) & (lane < (skip + count) * LANES)
         u = jnp.where(kept, a * jax.nn.sigmoid(a) * b, 0.0).astype(BF16)
@@ -322,9 +338,10 @@
                 copy.wait_send()
 
 
-def write_kernel(dims, len_ref, x_ref, entry_ref, c0, c1, x_out, out0, out1, patch_b, sems):
+def write_kernel(dims, len_ref, x_ref, entry_ref, c0, c1, x_out, out0, out1, patch_b, x_sem, sems):
     layers, rows, entry_w, slots = dims
-    x_out[...] = x_ref[...]
+    x_copy = pltpu.make_async_copy(x_ref, x_out, x_sem.at[0])
+    x_copy.start()
     entry_t = entry_ref[...].T[:entry_w]
     caches, outs = (c0, c1), (out0, out1)
     for layer in range(layers):
@@ -349,6 +366,7 @@
     for layer in range(layers):
         for r in range(rows):
             pltpu.make_async_copy(caches[layer].at[r], outs[layer].at[r], sems.at[layer, r]).wait()
+    x_copy.wait()
 
 
 def solution(mesh):
@@ -398,7 +416,7 @@
                 pltpu.VMEM((ranks * rows, model), F32),
                 pltpu.VMEM((layers, ranks, rows, model), BF16),
                 pltpu.VMEM((layers, members, rows, model), BF16),
-                dma((13,)),
+                dma((10,)),
                 dma((3,)),
                 dma((layers,)),
                 dma((layers,)),
@@ -415,8 +433,8 @@
             name="write",
             out_shape=(jax.ShapeDtypeStruct(x.shape, BF16), jax.ShapeDtypeStruct(c0.shape, BF16), jax.ShapeDtypeStruct(c1.shape, BF16)),
             in_specs=[SMEM_SPEC, VMEM_SPEC, VMEM_SPEC, VMEM_SPEC, VMEM_SPEC],
-            out_specs=(VMEM_SPEC, HBM_SPEC, HBM_SPEC),
-            scratch_shapes=[pltpu.VMEM((layers, rows, lat + rope, OUT_CHUNK), BF16), dma((layers, rows))],
+            out_specs=(HBM_SPEC, HBM_SPEC, HBM_SPEC),
+            scratch_shapes=[pltpu.VMEM((layers, rows, lat + rope, OUT_CHUNK), BF16), dma((1,)), dma((layers, rows))],
             compiler_params=pltpu.CompilerParams(vmem_limit_bytes=24 * 2 ** 20),
             cost_estimate=pl.CostEstimate(flops=10 ** 6, bytes_accessed=20 * 10 ** 6, transcendentals=0),
         )(lengths, x_new, entries, held0, held1)

time: 49.9 us -> 44.8 us (0.90)
  Pallas kernels: 49.1 us -> 44 us
    pallas_call x1, Pallas kernels: 44.2 us -> 39.7 us  [local_step(): pl.pallas_call(functools.partial(step_kernel, dims), name='step', out_sha...]
    pallas_call x1, Pallas kernels: 4.86 us -> 4.27 us  [local_step(): pl.pallas_call(functools.partial(write_kernel, (layers, rows, lat + rope,...]
where the time goes in v3:
time: 44.8 us; the launch traced here: 44.7 us
  Pallas kernels  44 us (98%)
  between operations  0.66 us (1%)
    pallas_call x1, Pallas kernels, local_step(): pl.pallas_call(functools.partial(step_kernel, dims), name='step', out_sha...  39.7 us
    pallas_call x1, Pallas kernels, local_step(): pl.pallas_call(functools.partial(write_kernel, (layers, rows, lat + rope,...  4.27 us

profile of v3, /device:TPU:1, one launch (start us, length us, event | category | flops | bytes accessed | tf_op | source)
XLA Modules:
  0.0 44.7 jit_solution(4827911962021234521)
XLA Ops:
  0.6 0.0 copy-start
  0.6 39.7 %step.1 = (bf16[2,2560]{1,0:T(2,128)(2,1)S(1)}, f32[8,384]{1,0:T(8,128)S(1)}, bf16[2,288,4096]{2,1,0:T(8,128)(2,1)S(1)}, bf16[2,288,4096]{2,1,0:T(8,128)(2,1)S(1)}) custom-call(s32[2]{0:T(128)} %len_ref.3, f32[8,512]{1,0:T(8,128)} %constant.2.clone.lane_ref, bf16[2,2560]{1,0:T(2,128)(2,1)} %x_ref.1, f32[2,2560]{1,0:T(2,128)} %attn_g.1, f32[2,256]{1,0:T(2,128)} %kv_g.1, ...), custom_call_target="tpu_custom_call" | custom-call | flops 1000000000 | bytes 70000000 | tf_op jit(solution)/shard_map/step/pallas_call | solution.py:396
  40.4 0.0 copy-done
  40.4 4.3 %write.1 = (bf16[2,2560]{1,0:T(2,128)(2,1)}, bf16[2,288,4096]{2,1,0:T(8,128)(2,1)}, bf16[2,288,4096]{2,1,0:T(8,128)(2,1)}) custom-call(s32[2]{0:T(128)S(1)} %copy-done, bf16[2,2560]{1,0:T(2,128)(2,1)S(1)} %get-tuple-element.10.x_ref, f32[8,384]{1,0:T(8,128)S(1)} %get-tuple-element.11.entry_ref, bf16[2,288,4096]{2,1,0:T(8,128)(2,1)S(1)} %get-tuple-element.12.c0, ...), custom_call_target="tpu_custom_call" | custom-call | flops 1000000 | bytes 20000000 | tf_op jit(solution)/shard_map/write/pallas_call | solution.py:431
Async XLA Ops:
  0.6 39.8 %copy-start = (s32[2]{0:T(128)S(1)}, s32[2]{0:T(128)}, u32[]{:S(2)}) copy-start(s32[2]{0:T(128)} %len_ref.3) | copy-start | bytes 28

commit v4 on v3

--- a/solution.py
+++ b/solution.py
@@ -109,6 +109,7 @@
 
     qa_rows = w_qa.shape[1] // 2
     o_cuts = cuts(w_o.shape[1], 2)
+    out_cuts = cuts(w_down.shape[2], 2)
 
     def attn_loads(layer):
         pairs = [("dkv", w_dkv.at[layer], dkv_b)]
@@ -302,29 +303,37 @@
         kept = (lane >= skip * LANES) & (lane < (skip + count) * LANES)
         u = jnp.where(kept, a * jax.nn.sigmoid(a) * b, 0.0).astype(BF16)
         f_loads[2].wait()
-        partial = dot(u, down_b[...])
-        for q in range(ranks):
-            send_b[layer, q] = partial[q * rows:(q + 1) * rows].astype(BF16)
-        sum_b[layer, me] = send_b[layer, pos]
-
         returns = []
-        for k in range(1, members):
-            q, t = peer(k)
-            returns.append(pltpu.make_async_remote_copy(
-                src_ref=send_b.at[layer, q], dst_ref=sum_b.at[layer, me], send_sem=rs.at[layer, k - 1], recv_sem=rr.at[layer, k - 1],
-                device_id={"tp": t, "dp": dp_of(q)}, device_id_type=MESH))
-        for copy in returns:
-            copy.start()
+        for n, (at, size) in enumerate(out_cuts):
+            cut = pl.ds(at, size)
+            partial = dot(u, down_b[:, at:at + size])
+            for q in range(ranks):
+                send_b[layer, q, :, at:at + size] = partial[q * rows:(q + 1) * rows].astype(BF16)
+            sum_b[layer, me, :, at:at + size] = send_b[layer, pos, :, at:at + size]
+            piece = []
+            for k in range(1, members):
+                q, t = peer(k)
+                piece.append(pltpu.make_async_remote_copy(
+                    src_ref=send_b.at[layer, q, :, cut], dst_ref=sum_b.at[layer, me, :, cut],
+                    send_sem=rs.at[layer, n, k - 1], recv_sem=rr.at[layer, n, k - 1],
+                    device_id={"tp": t, "dp": dp_of(q)}, device_id_type=MESH))
+            for copy in piece:
+                copy.start()
+            returns.append(piece)
         if layer + 1 < layers:
             f_loads = ffn_loads(layer + 1)
-        for copy in returns:
-            copy.wait_recv()
-        total = sum_b[layer, 0].astype(F32)
-        for j in range(1, members):
-            total = total + sum_b[layer, j].astype(F32)
+        totals = []
+        for (at, size), piece in zip(out_cuts, returns):
+            for copy in piece:
+                copy.wait_recv()
+            total = sum_b[layer, 0, :, at:at + size].astype(F32)
+            for j in range(1, members):
+                total = total + sum_b[layer, j, :, at:at + size].astype(F32)
+            totals.append(total)
+        total = jnp.concatenate(totals, axis=1)
         x_new = (x_mid.astype(F32) + total).astype(BF16)
         x = x_new.astype(F32)
-        sends.append((swap, gathers, returns))
+        sends.append((swap, gathers, sum(returns, [])))
 
     x_out[...] = x_new
     for swap, gathers, returns in sends:
@@ -422,8 +431,8 @@
                 dma((layers,)),
                 dma((layers, ranks - 1, tp_size)),
                 dma((layers, ranks - 1)),
-                dma((layers, members - 1)),
-                dma((layers, members - 1)),
+                dma((layers, 2, members - 1)),
+                dma((layers, 2, members - 1)),
             ],
             compiler_params=pltpu.CompilerParams(collective_id=0, has_side_effects=True, vmem_limit_bytes=46 * 2 ** 20),
             cost_estimate=pl.CostEstimate(flops=10 ** 9, bytes_accessed=70 * 10 ** 6, transcendentals=4 * 10 ** 5),

time: 44.8 us -> 45.4 us (1.013)
  Pallas kernels: 44 us -> 44.5 us
    pallas_call x1, Pallas kernels: 39.7 us -> 40.3 us  [local_step(): pl.pallas_call(functools.partial(step_kernel, dims), name='step', out_sha...]
where the time goes in v4:
time: 45.4 us; the launch traced here: 45.2 us
  Pallas kernels  44.5 us (98%)
  between operations  0.66 us (1%)
    pallas_call x1, Pallas kernels, local_step(): pl.pallas_call(functools.partial(step_kernel, dims), name='step', out_sha...  40.3 us
    pallas_call x1, Pallas kernels, local_step(): pl.pallas_call(functools.partial(write_kernel, (layers, rows, lat + rope,...  4.27 us

profile of v4, /device:TPU:1, one launch (start us, length us, event | category | flops | bytes accessed | tf_op | source)
XLA Modules:
  0.0 45.2 jit_solution(4315587195099883277)
XLA Ops:
  0.6 0.0 copy-start
  0.6 40.3 %step.1 = (bf16[2,2560]{1,0:T(2,128)(2,1)S(1)}, f32[8,384]{1,0:T(8,128)S(1)}, bf16[2,288,4096]{2,1,0:T(8,128)(2,1)S(1)}, bf16[2,288,4096]{2,1,0:T(8,128)(2,1)S(1)}) custom-call(s32[2]{0:T(128)} %len_ref.3, f32[8,512]{1,0:T(8,128)} %constant.2.clone.lane_ref, bf16[2,2560]{1,0:T(2,128)(2,1)} %x_ref.1, f32[2,2560]{1,0:T(2,128)} %attn_g.1, f32[2,256]{1,0:T(2,128)} %kv_g.1, ...), custom_call_target="tpu_custom_call" | custom-call | flops 1000000000 | bytes 70000000 | tf_op jit(solution)/shard_map/step/pallas_call | solution.py:405
  40.9 0.0 copy-done
  40.9 4.3 %write.1 = (bf16[2,2560]{1,0:T(2,128)(2,1)}, bf16[2,288,4096]{2,1,0:T(8,128)(2,1)}, bf16[2,288,4096]{2,1,0:T(8,128)(2,1)}) custom-call(s32[2]{0:T(128)S(1)} %copy-done, bf16[2,2560]{1,0:T(2,128)(2,1)S(1)} %get-tuple-element.10.x_ref, f32[8,384]{1,0:T(8,128)S(1)} %get-tuple-element.11.entry_ref, bf16[2,288,4096]{2,1,0:T(8,128)(2,1)S(1)} %get-tuple-element.12.c0, ...), custom_call_target="tpu_custom_call" | custom-call | flops 1000000 | bytes 20000000 | tf_op jit(solution)/shard_map/write/pallas_call | solution.py:440
Async XLA Ops:
  0.6 40.3 %copy-start = (s32[2]{0:T(128)S(1)}, s32[2]{0:T(128)}, u32[]{:S(2)}) copy-start(s32[2]{0:T(128)} %len_ref.3) | copy-start | bytes 28
